TPU v7x, 32 devices: a whole 2x2x4 slice. The times are simulated.
32 devices in a mesh: amp: 32 (over z, y, x, core).
Axes of the slice: x: 2, y: 2, z: 4, core: 2. Of those that a mesh axis runs over, the one named last changes fastest.
Arguments:
- ket_state: float32 [2, 1048576], P(None, 'amp'), may hold values from -6 to 6
- observable: float32 [1048576], P('amp'), may hold values from -6 to 6
- angles: float32 [2, 3], replicated, may hold values from -3.140625 to 3.140625
- gate_kinds: int32 [2, 32], replicated, may hold values from 0 to 2
Outputs:
- bra_state: float32 [2, 1048576], P(None, 'amp')
- grads: float32 [2, 3], replicated
Inputs may be any that keep to these rules, and one draw needn't show every extreme that they name: `gate_kinds`: 0 and 1 name rotations about Y with angles[l, 0] and angles[l, 1], 2 a rotation about Z with angles[l, 2]; entries for qubits at or above the number of qubits are not used.
All inputs are finite; a program needn't handle non-finite values.
Results may differ from a plain program's by a relative error of at most 0.0003.
Values sent between devices are 32-bit elements; how exact they have to be, the bound alone decides.
No kernel may reach another device: no remote copies, remote signals or barrier semaphores. Data moves between devices by JAX's collectives and lax.ppermute only.
A program may use at most 128 MiB of HBM per device.

v0:
```python
import functools
import math

import jax
import jax.numpy as jnp
from jax import lax
from jax.experimental import pallas as pl
from jax.experimental.pallas import tpu as pltpu
from jax.sharding import PartitionSpec as P

LANE_BITS = 7
ROW_BITS = 10
TILE = 8


class Frame:
    def __init__(self, local_bits, global_bits):
        self.local_bits = local_bits
        self.global_bits = global_bits
        self.all_bits = local_bits + global_bits
        self.pivot = local_bits - 1 - global_bits
        self.tiles = 1 << (local_bits - ROW_BITS)
        self.rows = self.tiles * TILE
        self.group = 1 << global_bits
        self.chunk = self.rows // self.group
        self.chunked = self.rows % self.group == 0 and self.chunk % TILE == 0

    def first_map(self):
        return {q: ("local", q) if q < self.local_bits else ("device", q - self.local_bits)
                for q in range(self.all_bits)}

    def second_map(self):
        where = {q: ("local", q) for q in range(self.pivot)}
        where[self.local_bits - 1] = ("local", self.pivot)
        for k in range(self.global_bits):
            where[self.local_bits + k] = ("local", self.pivot + 1 + k)
            where[self.pivot if k == self.global_bits - 1 else self.pivot + 1 + k] = ("device", k)
        return where

    def moved_map(self):
        return {pos: self.pivot if pos == self.local_bits - 1 else pos
                for pos in range(self.pivot + 1, self.local_bits)}


def lane_iota():
    return lax.broadcasted_iota(jnp.int32, (TILE, 128), 1)


def sub_iota():
    return lax.broadcasted_iota(jnp.int32, (TILE, 128), 0)


def bit_of(pos):
    if pos < LANE_BITS:
        return lane_iota() >> pos & 1
    return sub_iota() >> (pos - LANE_BITS) & 1


def sign_of(pos):
    return (1 - 2 * bit_of(pos)).astype(jnp.float32)


def shift_up(x, pos):
    if pos < LANE_BITS:
        return pltpu.roll(x, 128 - (1 << pos), 1)
    return pltpu.roll(x, TILE - (1 << (pos - LANE_BITS)), 0)


def shift_down(x, pos):
    if pos < LANE_BITS:
        return pltpu.roll(x, 1 << pos, 1)
    return pltpu.roll(x, 1 << (pos - LANE_BITS), 0)


def flip(x, pos):
    if pos in (LANE_BITS - 1, ROW_BITS - 1):
        return shift_down(x, pos)
    return jnp.where(bit_of(pos) == 0, shift_up(x, pos), shift_down(x, pos))


def entangle(amp, all_bits):
    x = amp & (amp >> 1 | (amp & 1) << (all_bits - 1))
    step = 16
    while step:
        x = x ^ x >> step
        step //= 2
    return (1 - 2 * (x & 1)).astype(jnp.float32)


def position_index(tile):
    return tile << ROW_BITS | sub_iota() << LANE_BITS | lane_iota()


def swap_pivot(tiles, frame):
    half = len(tiles) // 2
    pos = frame.pivot
    out = list(tiles)
    for t in range(half):
        low, high = tiles[t], tiles[t + half]
        if pos >= ROW_BITS:
            bit = 1 << (pos - ROW_BITS)
            if t & bit:
                out[t], out[t - bit + half] = tiles[t - bit + half], tiles[t]
        else:
            keep = bit_of(pos) == 0
            out[t] = jnp.where(keep, low, shift_down(high, pos))
            out[t + half] = jnp.where(keep, shift_up(low, pos), high)
    return out


class Params:
    def __init__(self, table, kinds, layers):
        self.table = table
        self.kinds = kinds
        self.layers = layers

    def gate(self, layer, qubit):
        return (self.table[layer, qubit], self.table[self.layers + layer, qubit],
                self.table[2 * self.layers + layer, qubit])

    def pick(self, layer, qubit, kind):
        return jnp.where(self.kinds[layer, qubit] == kind, 0.5, 0.0)


def turn(re, im, gate, pos, low_tile_bit):
    c, sy, sz = gate
    if pos < ROW_BITS:
        z = sign_of(pos)
        y_part, z_part = sy * z, sz * z
        new_re = [c * a + y_part * flip(a, pos) - z_part * b for a, b in zip(re, im)]
        new_im = [c * b + y_part * flip(b, pos) + z_part * a for a, b in zip(re, im)]
        return new_re, new_im
    bit = 1 << (pos - ROW_BITS - low_tile_bit)
    new_re, new_im = list(re), list(im)
    for t in range(len(re)):
        if t & bit:
            continue
        u = t | bit
        new_re[t] = c * re[t] + sy * re[u] - sz * im[t]
        new_im[t] = c * im[t] + sy * im[u] + sz * re[t]
        new_re[u] = c * re[u] - sy * re[t] + sz * im[u]
        new_im[u] = c * im[u] - sy * im[t] - sz * re[u]
    return new_re, new_im


def sweep(loads, stores, frame, gates):
    tile_bits = frame.tiles.bit_length() - 1
    low = min(3, tile_bits)
    span = 1 << low
    near = [pos for pos in sorted(gates) if LANE_BITS <= pos < ROW_BITS + low]
    far = [pos for pos in sorted(gates) if pos >= ROW_BITS + low]
    load, store = loads, stores
    plans = []
    if near:
        plans.append((near, 0, [[base * span + t for t in range(span)]
                                for base in range(frame.tiles // span)]))
    if far:
        plans.append((far, low, [[base + t * span for t in range(frame.tiles // span)]
                                 for base in range(span)]))
    for positions, low_bit, blocks in plans:
        for block in blocks:
            pairs = [load(t) for t in block]
            re, im = [a for a, _ in pairs], [b for _, b in pairs]
            for pos in positions:
                re, im = turn(re, im, gates[pos], pos, low_bit)
            for t, a, b in zip(block, re, im):
                store(t, a, b)


def split(x):
    high = x.astype(jnp.bfloat16)
    return high, (x - high.astype(jnp.float32)).astype(jnp.bfloat16)


def lane_matrix(params, layer, qubits):
    into = lax.broadcasted_iota(jnp.int32, (128, 128), 0)
    out = lax.broadcasted_iota(jnp.int32, (128, 128), 1)
    real = imag = None
    for pos, qubit in enumerate(qubits):
        c, sy, sz = params.gate(layer, qubit)
        z = (1 - 2 * (out >> pos & 1)).astype(jnp.float32)
        same = (into ^ out) >> pos & 1 == 0
        g_real = jnp.where(same, c, sy * z)
        g_imag = jnp.where(same, sz * z, 0.0)
        if real is None:
            real, imag = g_real, g_imag
        else:
            real, imag = real * g_real - imag * g_imag, real * g_imag + imag * g_real
    top = jnp.concatenate([real, imag], axis=1)
    bottom = jnp.concatenate([-imag, real], axis=1)
    return jnp.concatenate([top, bottom], axis=0)


def lane_turn(x, matrix):
    x_high, x_low = split(x)
    m_high, m_low = split(matrix)
    dot = functools.partial(jnp.dot, preferred_element_type=jnp.float32)
    return dot(x_high, m_high) + (dot(x_low, m_high) + dot(x_high, m_low))


def parts_of(where, qubit, device):
    kind, pos = where[qubit]
    if kind == "device":
        return None, None, (1 - 2 * (device >> pos & 1)).astype(jnp.float32)
    if pos >= ROW_BITS:
        return 1 << (pos - ROW_BITS), None, None
    return None, sign_of(pos), None


def odd(x):
    return bin(x).count("1") & 1


def gather_terms(frame, where, qubits, load_ket, load_bra, params, device):
    n = frame.all_bits
    layers = params.layers
    zero = jnp.zeros((TILE, 128), jnp.float32)
    near, far = [], []
    for q in qubits:
        (far if where[q][1] >= ROW_BITS else near).append(q)
    ratio_mask = {}
    for q in qubits:
        mask = 0
        for other in ((q - 1) % n, (q + 1) % n):
            kind, pos = where[other]
            if kind == "local" and pos >= ROW_BITS:
                mask ^= 1 << (pos - ROW_BITS)
        ratio_mask[q] = mask
    buckets = {q: [None, None] for q in qubits}

    def add(q, side, value):
        old = buckets[q][side]
        buckets[q][side] = value if old is None else old + value

    phases = []
    for t in range(frame.tiles):
        ket_re, ket_im = load_ket(t)
        bra_re, bra_im = load_bra(t)
        phases.append(bra_re * ket_im - bra_im * ket_re)
        for q in near:
            pos = where[q][1]
            value = bra_re * flip(ket_re, pos) + bra_im * flip(ket_im, pos)
            add(q, odd(t & ratio_mask[q]), value)
    for q in far:
        bit = 1 << (where[q][1] - ROW_BITS)
        for t in range(frame.tiles):
            if t & bit:
                continue
            ket_low, ket_high = load_ket(t), load_ket(t | bit)
            bra_low, bra_high = load_bra(t), load_bra(t | bit)
            value = (bra_high[0] * ket_low[0] + bra_high[1] * ket_low[1]) - (
                bra_low[0] * ket_high[0] + bra_low[1] * ket_high[1])
            add(q, odd(t & ratio_mask[q]), value)
    signed = {}
    level = phases
    bit = frame.tiles // 2
    while bit:
        diffs = [level[t] - level[t + bit] for t in range(bit)]
        while len(diffs) > 1:
            half = len(diffs) // 2
            diffs = [diffs[t] + diffs[t + half] for t in range(half)]
        signed[bit] = diffs[0]
        level = [level[t] + level[t + bit] for t in range(bit)]
        bit //= 2
    total = level[0]
    sums = [[zero, zero, zero] for _ in range(layers)]
    for q in qubits:
        pos = where[q][1]
        plus, minus = [zero if b is None else b for b in buckets[q]]
        if pos < ROW_BITS:
            z = sign_of(pos)
            phase = total * z
            last = (plus + minus) * -z
            first = (plus - minus) * -z
        else:
            phase = signed[1 << (pos - ROW_BITS)]
            last = plus + minus
            first = plus - minus
        for other in ((q - 1) % n, (q + 1) % n):
            _, vector, scalar = parts_of(where, other, device)
            if vector is not None:
                first = first * vector
            if scalar is not None:
                first = first * scalar
        for layer in range(layers):
            y_term = last if layer == layers - 1 else first
            for kind in range(2):
                sums[layer][kind] = sums[layer][kind] + params.pick(layer, q, kind) * y_term
            sums[layer][2] = sums[layer][2] + params.pick(layer, q, 2) * phase
    return sums


def rows_of(sums):
    flat = [jnp.sum(tile, axis=0, keepdims=True) for layer in sums for tile in layer]
    flat += [jnp.zeros((1, 128), jnp.float32)] * (TILE - len(flat))
    return jnp.concatenate(flat, axis=0)


def tile_ref(frame, ref, comp, comps):
    def at(t):
        if frame.chunked:
            per = frame.chunk // TILE
            start = comp * frame.chunk + t % per * TILE
            return (t // per, pl.ds(start, TILE), slice(None))
        return (comp, pl.ds(t * TILE, TILE), slice(None))
    return at


def scratch_io(ref, frame, state):
    base = state * frame.rows

    def load(t):
        rows = pl.ds(base + t * TILE, TILE)
        return ref[rows, 0:128], ref[rows, 128:256]

    def store(t, re, im):
        rows = pl.ds(base + t * TILE, TILE)
        ref[rows, 0:128] = re
        ref[rows, 128:256] = im

    return load, store


def first_kernel(frame, layers, dev_ref, table, kinds, ket_ref, obs_ref, out_ref, sums_ref, work):
    device = dev_ref[0]
    params = Params(table, kinds, layers)
    layer = layers - 1
    scale = 2.0 / math.sqrt(1 << frame.all_bits)
    load_ket, store_ket = scratch_io(work, frame, 0)
    load_bra, store_bra = scratch_io(work, frame, 1)
    for t in range(frame.tiles):
        sign = entangle(device << frame.local_bits | position_index(t), frame.all_bits)
        re = ket_ref[pl.ds(2 * TILE * t, TILE, stride=2), :] * sign
        im = ket_ref[pl.ds(2 * TILE * t + 1, TILE, stride=2), :] * sign
        store_ket(t, re, im)
        factor = obs_ref[pl.ds(TILE * t, TILE), :] * scale
        store_bra(t, re * factor, im * factor)
    work[...] = lane_turn(work[...], lane_matrix(params, layer, range(LANE_BITS)))
    gates = {pos: params.gate(layer, pos) for pos in range(LANE_BITS, frame.local_bits)}
    sweep(load_ket, store_ket, frame, gates)
    sweep(load_bra, store_bra, frame, gates)
    moved = list(range(frame.pivot, frame.local_bits - 1))
    sums = gather_terms(frame, frame.first_map(), moved, load_ket, load_bra, params, device)
    sums_ref[...] = rows_of(sums)
    for state, load in enumerate((load_ket, load_bra)):
        pairs = [load(t) for t in range(frame.tiles)]
        for part in range(2):
            tiles = swap_pivot([pair[part] for pair in pairs], frame)
            at = tile_ref(frame, out_ref, 2 * state + part, 4)
            for t in range(frame.tiles):
                out_ref[at(t)] = tiles[t]


def middle_kernel(frame, layers, dev_ref, table, kinds, in_ref, sums_ref, out_ref, work, *flat_out):
    device = dev_ref[0]
    params = Params(table, kinds, layers)
    load_ket, store_ket = scratch_io(work, frame, 0)
    load_bra, store_bra = scratch_io(work, frame, 1)
    where = frame.second_map()
    placed = {pos: q for q, (kind, pos) in where.items() if kind == "local"}
    at = [tile_ref(frame, in_ref, comp, 4) for comp in range(4)]
    for t in range(frame.tiles):
        store_ket(t, in_ref[at[0](t)], in_ref[at[1](t)])
        store_bra(t, in_ref[at[2](t)], in_ref[at[3](t)])
    lane_gates = [pos for pos in range(frame.pivot + 1, frame.local_bits) if pos < LANE_BITS]
    assert not lane_gates
    gates = {pos: params.gate(layers - 1, placed[pos])
             for pos in range(frame.pivot + 1, frame.local_bits)}
    sweep(load_ket, store_ket, frame, gates)
    sweep(load_bra, store_bra, frame, gates)
    qubits = [placed[pos] for pos in range(frame.local_bits)]
    sums = gather_terms(frame, where, qubits, load_ket, load_bra, params, device)
    partial = sums_ref[...] + rows_of(sums)
    g = frame.global_bits
    high = device >> (g - 1) & 1
    base = (device & (1 << (g - 1)) - 1) << (frame.pivot + 1) | high << frame.pivot
    for t in range(frame.tiles):
        pos = position_index(t)
        amp = (base | pos & (1 << frame.pivot) - 1
               | (pos >> frame.pivot & 1) << (frame.local_bits - 1)
               | pos >> (frame.pivot + 1) << frame.local_bits)
        sign = entangle(amp, frame.all_bits)
        re, im = load_bra(t)
        store_bra(t, re * sign, im * sign)
    bra_rows = pl.ds(frame.rows, frame.rows)
    lane_qubits = [placed[pos] for pos in range(LANE_BITS)]
    lane_on = [placed[pos] for pos in range(LANE_BITS)]
    work[bra_rows, :] = lane_turn(work[bra_rows, :], lane_matrix(params, 0, lane_on))
    gates = {pos: params.gate(0, placed[pos]) for pos in range(LANE_BITS, frame.local_bits)}
    sweep(load_bra, store_bra, frame, gates)
    at = [tile_ref(frame, out_ref, comp, 2) for comp in range(2)]
    for t in range(frame.tiles):
        re, im = load_bra(t)
        out_ref[at[0](t)] = re
        out_ref[at[1](t)] = im
    if frame.chunked:
        for j in range(frame.group):
            out_ref[j, pl.ds(2 * frame.chunk, TILE), :] = partial
    else:
        flat_out[0][...] = partial


def last_kernel(frame, layers, table, kinds, in_ref, sums_ref, bra_ref, grads_ref, work):
    params = Params(table, kinds, layers)
    load, store = scratch_io(work, frame, 0)
    at = [tile_ref(frame, in_ref, comp, 2) for comp in range(2)]
    for t in range(frame.tiles):
        store(t, in_ref[at[0](t)], in_ref[at[1](t)])
    gates = {pos: params.gate(0, q) for pos, q in frame.moved_map().items()}
    sweep(load, store, frame, gates)
    pairs = [load(t) for t in range(frame.tiles)]
    for part in range(2):
        tiles = swap_pivot([pair[part] for pair in pairs], frame)
        for t in range(frame.tiles):
            bra_ref[pl.ds(2 * TILE * t + part, TILE, stride=2), :] = tiles[t]
    total = None
    for j in range(frame.group):
        part = in_ref[j, pl.ds(2 * frame.chunk, TILE), :] if frame.chunked else sums_ref[j]
        total = part if total is None else total + part
    for layer in range(layers):
        for kind in range(3):
            row = 3 * layer + kind
            grads_ref[layer, kind] = jnp.sum(total[row:row + 1, :])


def on_device(ket_state, observable, angles, gate_kinds):
    amp_count = ket_state.shape[1]
    local_bits = amp_count.bit_length() - 1
    group = lax.axis_size("amp")
    frame = Frame(local_bits, group.bit_length() - 1)
    layers = angles.shape[0]
    rows = frame.rows
    device = lax.axis_index("amp").astype(jnp.int32).reshape(1)
    chosen = gate_kinds[:, :, None] == jnp.arange(angles.shape[1])[None, None, :]
    half = 0.5 * jnp.sum(jnp.where(chosen, angles[:, None, :], 0.0), axis=-1)
    cosine, sine = jnp.cos(half), jnp.sin(half)
    is_z = gate_kinds == 2
    table = jnp.concatenate(
        [cosine, jnp.where(is_z, 0.0, sine), jnp.where(is_z, sine, 0.0)], axis=0)
    smem = pl.BlockSpec(memory_space=pltpu.SMEM)
    vmem = pl.BlockSpec(memory_space=pltpu.VMEM)
    f32 = jnp.float32

    def packed(comps, extra):
        if frame.chunked:
            return jax.ShapeDtypeStruct((group, comps * frame.chunk + extra, 128), f32)
        return jax.ShapeDtypeStruct((comps, rows, 128), f32)

    def exchange(x):
        return lax.all_to_all(x, "amp", 0, 0, tiled=True)

    def to_chunks(x):
        comps = x.shape[0]
        return x.reshape(comps, group, rows * 128 // group).transpose(1, 0, 2)

    def from_chunks(x):
        return x.transpose(1, 0, 2).reshape(x.shape[1], rows, 128)

    ket_rows = ket_state.reshape(2, rows, 128).transpose(1, 0, 2).reshape(2 * rows, 128)
    obs_rows = observable.reshape(rows, 128)
    work = pltpu.VMEM((2 * rows, 256), f32)
    tile = jax.ShapeDtypeStruct((TILE, 128), f32)
    sent, sums = pl.pallas_call(
        functools.partial(first_kernel, frame, layers),
        in_specs=[smem, smem, smem, vmem, vmem],
        out_specs=(vmem, vmem),
        out_shape=(packed(4, 0), tile),
        scratch_shapes=[work],
        name="first_kernel",
    )(device, table, gate_kinds, ket_rows, obs_rows)
    if frame.chunked:
        got = exchange(sent)
    else:
        got = from_chunks(exchange(to_chunks(sent)))
    outs = (packed(2, TILE),) if frame.chunked else (packed(2, TILE), tile)
    back = pl.pallas_call(
        functools.partial(
            middle_kernel if frame.chunked else middle_flat, frame, layers),
        in_specs=[smem, smem, smem, vmem, vmem],
        out_specs=(vmem,) * len(outs),
        out_shape=outs,
        scratch_shapes=[work],
        name="middle_kernel",
    )(device, table, gate_kinds, got, sums)
    if frame.chunked:
        final = exchange(back[0])
        parts = jnp.zeros((1, TILE, 128), f32)
    else:
        final = from_chunks(exchange(to_chunks(back[0])))
        parts = lax.all_gather(back[1], "amp")
    bra_rows, grads = pl.pallas_call(
        functools.partial(last_kernel, frame, layers),
        in_specs=[smem, smem, vmem, vmem],
        out_specs=(vmem, smem),
        out_shape=(jax.ShapeDtypeStruct((2 * rows, 128), f32),
                   jax.ShapeDtypeStruct((layers, 3), f32)),
        scratch_shapes=[pltpu.VMEM((rows, 256), f32)],
        name="last_kernel",
    )(table, gate_kinds, final, parts)
    bra = bra_rows.reshape(rows, 2, 128).transpose(1, 0, 2).reshape(2, amp_count)
    return bra, grads


def middle_flat(frame, layers, dev_ref, table, kinds, in_ref, sums_ref, out_ref, part_ref, work):
    middle_kernel(frame, layers, dev_ref, table, kinds, in_ref, sums_ref, out_ref, work, part_ref)


def solution(mesh):
    placed = (P(None, "amp"), P("amp"), P(), P())
    return jax.shard_map(
        on_device, mesh=mesh, in_specs=placed, out_specs=(P(None, "amp"), P()), check_vma=False
    )
```

profile of v0, /device:TPU:0, one launch (start us, length us, event | category | flops | bytes accessed | tf_op | source)
XLA Modules:
  0.0 51.8 jit_solution(16930777060487112208)
XLA Ops:
  0.6 0.0 copy-start.1
  0.6 0.7 %copy-done.1 = f32[2,3]{1,0:T(2,128)S(1)} copy-done((f32[2,3]{1,0:T(2,128)S(1)}, f32[2,3]{1,0:T(2,128)}, u32[]{:S(2)}) %copy-start.1) | copy-done | bytes 48
  1.3 0.0 copy-start
  1.3 0.1 copy.8
  1.4 0.6 %copy-done = s32[2,32]{1,0:T(2,128)S(1)} copy-done((s32[2,32]{1,0:T(2,128)S(1)}, s32[2,32]{1,0:T(2,128)}, u32[]{:S(2)}) %copy-start) | copy-done | bytes 280
  2.0 0.1 fusion
  2.1 0.6 %pad_maximum_fusion.table = f32[6,32]{1,0:T(8,128)} fusion(f32[2,32]{1,0:T(2,128)S(1)} %get-tuple-element.11, f32[2,32]{1,0:T(2,128)S(1)} %get-tuple-element.10, f32[2,32]{1,0:T(2,128)S(1)} %get-tuple-element.12), kind=kLoop, calls=%fused_computation.1 | loop fusion | flops 384 | bytes 1536 | tf_op jit(solution)/shard_map/concatenate | solution.py:438
  2.7 3.2 %first_kernel.1 = (f32[32,32,128]{2,1,0:T(8,128)}, f32[8,128]{1,0:T(8,128)}) custom-call(s32[1]{0:T(128)} %bitcast.dev_ref, f32[6,32]{1,0:T(8,128)} %pad_maximum_fusion.table, s32[2,32]{1,0:T(2,128)} %kinds.5, f32[512,128]{1,0:T(8,128)} %bitcast.12, f32[256,128]{1,0:T(8,128)} %bitcast.13), custom_call_target="tpu_custom_call" | custom-call | tf_op jit(solution)/shard_map/first_kernel/pallas_call | solution.py:463
  5.9 23.1 %all_to_all.10.in_ref = f32[32,32,128]{2,1,0:T(8,128)} all-to-all(f32[32,32,128]{2,1,0:T(8,128)} %get-tuple-element.6), channel_id=1, replica_groups=mesh['amp'=32] {'amp'}, dimensions={0} | all-to-all | bytes 1048576 | tf_op jit(solution)/shard_map/all_to_all | solution.py:450
  29.0 3.7 %middle_kernel.1 = f32[32,24,128]{2,1,0:T(8,128)} custom-call(s32[1]{0:T(128)} %bitcast.dev_ref, f32[6,32]{1,0:T(8,128)} %pad_maximum_fusion.table, s32[2,32]{1,0:T(2,128)} %kinds.5, f32[32,32,128]{2,1,0:T(8,128)} %all_to_all.10.in_ref, f32[8,128]{1,0:T(8,128)} %get-tuple-element.7.sums_ref), custom_call_target="tpu_custom_call" | custom-call | tf_op jit(solution)/shard_map/middle_kernel/pallas_call | solution.py:476
  32.6 16.5 %all_to_all.11.in_ref = f32[32,24,128]{2,1,0:T(8,128)} all-to-all(f32[32,24,128]{2,1,0:T(8,128)} %middle_kernel.1), channel_id=1, replica_groups=mesh['amp'=32] {'amp'}, dimensions={0} | all-to-all | bytes 786432 | tf_op jit(solution)/shard_map/all_to_all | solution.py:450
  49.2 0.6 %broadcast_in_dim.27.sums_ref = f32[1,8,128]{2,1,0:T(8,128)} broadcast(f32[]{:T(128)} %constant.4.clone.1), dimensions={} | broadcast | bytes 4100 | tf_op jit(solution)/shard_map/broadcast_in_dim | solution.py:487
  49.8 2.0 %last_kernel.1 = (f32[512,128]{1,0:T(8,128)}, f32[2,3]{1,0:T(2,128)}) custom-call(f32[6,32]{1,0:T(8,128)} %pad_maximum_fusion.table, s32[2,32]{1,0:T(2,128)} %kinds.5, f32[32,24,128]{2,1,0:T(8,128)} %all_to_all.11.in_ref, f32[1,8,128]{2,1,0:T(8,128)} %broadcast_in_dim.27.sums_ref), custom_call_target="tpu_custom_call" | custom-call | tf_op jit(solution)/shard_map/last_kernel/pallas_call | solution.py:491
  (1 shorter events, 0.0 us)
Async XLA Ops:
  0.6 0.7 %copy-start.1 = (f32[2,3]{1,0:T(2,128)S(1)}, f32[2,3]{1,0:T(2,128)}, u32[]{:S(2)}) copy-start(f32[2,3]{1,0:T(2,128)} %param.6) | copy-start | bytes 76
  1.3 0.7 %copy-start = (s32[2,32]{1,0:T(2,128)S(1)}, s32[2,32]{1,0:T(2,128)}, u32[]{:S(2)}) copy-start(s32[2,32]{1,0:T(2,128)} %kinds.5) | copy-start | bytes 772
where the time goes:
time: 52.2 us; the launch traced here: 51.8 us
  blocking collectives  39.6 us (76%)
  Pallas kernels  8.86 us (17%)
  local copies, waits for them, and re-layouts  1.94 us (4%)
  other arithmetic  0.73 us (1%)
  between operations  0.65 us (1%)
    all_to_all x2, blocking collectives, exchange(): return lax.all_to_all(x, 'amp', 0, 0, tiled=True)  39.6 us
    pallas_call x1, Pallas kernels, on_device(): pl.pallas_call(functools.partial(middle_kernel if frame.chunked else midd...  3.68 us
    pallas_call x1, Pallas kernels, on_device(): pl.pallas_call(functools.partial(first_kernel, frame, layers), in_specs=[...  3.19 us
    pallas_call x1, Pallas kernels, on_device(): pl.pallas_call(functools.partial(last_kernel, frame, layers), in_specs=[s...  1.98 us
    unnamed x5, local copies, waits for them, and re-layouts  1.35 us

commit v1 on v0

--- a/solution.py
+++ b/solution.py
@@ -108,15 +108,40 @@
     return out
 
 
+def polynomial(x, coefficients):
+    total = jnp.full_like(x, coefficients[-1])
+    for value in coefficients[-2::-1]:
+        total = total * x + value
+    return total
+
+
+def half_turn(angle):
+    x = jnp.full((TILE, 128), 0.5, jnp.float32) * angle
+    square = x * x
+    cosine = polynomial(square, [(-1) ** k / math.factorial(2 * k) for k in range(9)])
+    sine = x * polynomial(square, [(-1) ** k / math.factorial(2 * k + 1) for k in range(8)])
+    return cosine, sine
+
+
 class Params:
-    def __init__(self, table, kinds, layers):
-        self.table = table
+    def __init__(self, angles, kinds, layers):
         self.kinds = kinds
         self.layers = layers
+        self.turns = {}
+        self.angles = angles
+
+    def turn(self, layer, kind):
+        if (layer, kind) not in self.turns:
+            self.turns[layer, kind] = half_turn(self.angles[layer, kind])
+        return self.turns[layer, kind]
 
     def gate(self, layer, qubit):
-        return (self.table[layer, qubit], self.table[self.layers + layer, qubit],
-                self.table[2 * self.layers + layer, qubit])
+        kind = self.kinds[layer, qubit]
+        (c0, s0), (c1, s1), (c2, s2) = [self.turn(layer, k) for k in range(3)]
+        is_z = kind == 2
+        c = jnp.where(is_z, c2, jnp.where(kind == 1, c1, c0))
+        sy = jnp.where(is_z, 0.0, jnp.where(kind == 1, s1, s0))
+        return c, sy, jnp.where(is_z, s2, 0.0)
 
     def pick(self, layer, qubit, kind):
         return jnp.where(self.kinds[layer, qubit] == kind, 0.5, 0.0)
@@ -177,7 +202,7 @@
     out = lax.broadcasted_iota(jnp.int32, (128, 128), 1)
     real = imag = None
     for pos, qubit in enumerate(qubits):
-        c, sy, sz = params.gate(layer, qubit)
+        c, sy, sz = [jnp.concatenate([v] * 16, axis=0) for v in params.gate(layer, qubit)]
         z = (1 - 2 * (out >> pos & 1)).astype(jnp.float32)
         same = (into ^ out) >> pos & 1 == 0
         g_real = jnp.where(same, c, sy * z)
@@ -290,13 +315,29 @@
     return sums
 
 
+def one_row(tile):
+    for step in (64, 32, 16):
+        tile = tile + pltpu.roll(tile, step, 1)
+    return jnp.sum(jnp.where(lane_iota() >> 4 == sub_iota(), tile, 0.0), axis=0, keepdims=True)
+
+
 def rows_of(sums):
     flat = [jnp.sum(tile, axis=0, keepdims=True) for layer in sums for tile in layer]
     flat += [jnp.zeros((1, 128), jnp.float32)] * (TILE - len(flat))
     return jnp.concatenate(flat, axis=0)
 
 
-def tile_ref(frame, ref, comp, comps):
+def back_ref(frame, comp):
+    def at(t):
+        if frame.chunked:
+            per = frame.chunk // TILE
+            start = t // per * (2 * frame.chunk + 1) + comp * frame.chunk + t % per * TILE
+            return (pl.ds(start, TILE), slice(None))
+        return (comp, pl.ds(t * TILE, TILE), slice(None))
+    return at
+
+
+def tile_ref(frame, comp):
     def at(t):
         if frame.chunked:
             per = frame.chunk // TILE
@@ -321,9 +362,9 @@
     return load, store
 
 
-def first_kernel(frame, layers, dev_ref, table, kinds, ket_ref, obs_ref, out_ref, sums_ref, work):
+def first_kernel(frame, layers, dev_ref, angles, kinds, ket_ref, obs_ref, out_ref, sums_ref, work):
     device = dev_ref[0]
-    params = Params(table, kinds, layers)
+    params = Params(angles, kinds, layers)
     layer = layers - 1
     scale = 2.0 / math.sqrt(1 << frame.all_bits)
     load_ket, store_ket = scratch_io(work, frame, 0)
@@ -346,31 +387,30 @@
         pairs = [load(t) for t in range(frame.tiles)]
         for part in range(2):
             tiles = swap_pivot([pair[part] for pair in pairs], frame)
-            at = tile_ref(frame, out_ref, 2 * state + part, 4)
+            at = tile_ref(frame, 2 * state + part)
             for t in range(frame.tiles):
                 out_ref[at(t)] = tiles[t]
 
 
-def middle_kernel(frame, layers, dev_ref, table, kinds, in_ref, sums_ref, out_ref, work, *flat_out):
+def middle_kernel(frame, layers, dev_ref, angles, kinds, in_ref, sums_ref, out_ref, work, *flat_out):
     device = dev_ref[0]
-    params = Params(table, kinds, layers)
+    params = Params(angles, kinds, layers)
     load_ket, store_ket = scratch_io(work, frame, 0)
     load_bra, store_bra = scratch_io(work, frame, 1)
     where = frame.second_map()
     placed = {pos: q for q, (kind, pos) in where.items() if kind == "local"}
-    at = [tile_ref(frame, in_ref, comp, 4) for comp in range(4)]
+    at = [tile_ref(frame, comp) for comp in range(4)]
     for t in range(frame.tiles):
         store_ket(t, in_ref[at[0](t)], in_ref[at[1](t)])
         store_bra(t, in_ref[at[2](t)], in_ref[at[3](t)])
-    lane_gates = [pos for pos in range(frame.pivot + 1, frame.local_bits) if pos < LANE_BITS]
-    assert not lane_gates
+    assert frame.pivot + 1 >= LANE_BITS
     gates = {pos: params.gate(layers - 1, placed[pos])
              for pos in range(frame.pivot + 1, frame.local_bits)}
     sweep(load_ket, store_ket, frame, gates)
     sweep(load_bra, store_bra, frame, gates)
     qubits = [placed[pos] for pos in range(frame.local_bits)]
     sums = gather_terms(frame, where, qubits, load_ket, load_bra, params, device)
-    partial = sums_ref[...] + rows_of(sums)
+    partial = one_row(sums_ref[...] + rows_of(sums))
     g = frame.global_bits
     high = device >> (g - 1) & 1
     base = (device & (1 << (g - 1)) - 1) << (frame.pivot + 1) | high << frame.pivot
@@ -383,27 +423,28 @@
         re, im = load_bra(t)
         store_bra(t, re * sign, im * sign)
     bra_rows = pl.ds(frame.rows, frame.rows)
-    lane_qubits = [placed[pos] for pos in range(LANE_BITS)]
     lane_on = [placed[pos] for pos in range(LANE_BITS)]
     work[bra_rows, :] = lane_turn(work[bra_rows, :], lane_matrix(params, 0, lane_on))
     gates = {pos: params.gate(0, placed[pos]) for pos in range(LANE_BITS, frame.local_bits)}
     sweep(load_bra, store_bra, frame, gates)
-    at = [tile_ref(frame, out_ref, comp, 2) for comp in range(2)]
+    at = [back_ref(frame, comp) for comp in range(2)]
     for t in range(frame.tiles):
         re, im = load_bra(t)
         out_ref[at[0](t)] = re
         out_ref[at[1](t)] = im
     if frame.chunked:
         for j in range(frame.group):
-            out_ref[j, pl.ds(2 * frame.chunk, TILE), :] = partial
+            row = (j + 1) * (2 * frame.chunk + 1) - 1
+            out_ref[pl.ds(row, 1), :] = partial
     else:
         flat_out[0][...] = partial
 
 
-def last_kernel(frame, layers, table, kinds, in_ref, sums_ref, bra_ref, grads_ref, work):
-    params = Params(table, kinds, layers)
+def last_kernel(frame, layers, angles, kinds, in_ref, *refs):
+    *sums_ref, bra_ref, grads_ref, work = refs
+    params = Params(angles, kinds, layers)
     load, store = scratch_io(work, frame, 0)
-    at = [tile_ref(frame, in_ref, comp, 2) for comp in range(2)]
+    at = [back_ref(frame, comp) for comp in range(2)]
     for t in range(frame.tiles):
         store(t, in_ref[at[0](t)], in_ref[at[1](t)])
     gates = {pos: params.gate(0, q) for pos, q in frame.moved_map().items()}
@@ -413,14 +454,17 @@
         tiles = swap_pivot([pair[part] for pair in pairs], frame)
         for t in range(frame.tiles):
             bra_ref[pl.ds(2 * TILE * t + part, TILE, stride=2), :] = tiles[t]
-    total = None
-    for j in range(frame.group):
-        part = in_ref[j, pl.ds(2 * frame.chunk, TILE), :] if frame.chunked else sums_ref[j]
-        total = part if total is None else total + part
+    if frame.chunked:
+        step = 2 * frame.chunk + 1
+        rows = in_ref[pl.ds(step - 1, frame.group, stride=step), :]
+    else:
+        rows = sums_ref[0][:, 0, :]
+    total = jnp.sum(rows, axis=0, keepdims=True)
+    owner = lax.broadcasted_iota(jnp.int32, (1, 128), 1) >> 4
     for layer in range(layers):
         for kind in range(3):
-            row = 3 * layer + kind
-            grads_ref[layer, kind] = jnp.sum(total[row:row + 1, :])
+            own = jnp.where(owner == 3 * layer + kind, total, 0.0)
+            grads_ref[layer, kind] = jnp.sum(own)
 
 
 def on_device(ket_state, observable, angles, gate_kinds):
@@ -431,19 +475,11 @@
     layers = angles.shape[0]
     rows = frame.rows
     device = lax.axis_index("amp").astype(jnp.int32).reshape(1)
-    chosen = gate_kinds[:, :, None] == jnp.arange(angles.shape[1])[None, None, :]
-    half = 0.5 * jnp.sum(jnp.where(chosen, angles[:, None, :], 0.0), axis=-1)
-    cosine, sine = jnp.cos(half), jnp.sin(half)
-    is_z = gate_kinds == 2
-    table = jnp.concatenate(
-        [cosine, jnp.where(is_z, 0.0, sine), jnp.where(is_z, sine, 0.0)], axis=0)
     smem = pl.BlockSpec(memory_space=pltpu.SMEM)
     vmem = pl.BlockSpec(memory_space=pltpu.VMEM)
     f32 = jnp.float32
 
-    def packed(comps, extra):
-        if frame.chunked:
-            return jax.ShapeDtypeStruct((group, comps * frame.chunk + extra, 128), f32)
+    def flat(comps):
         return jax.ShapeDtypeStruct((comps, rows, 128), f32)
 
     def exchange(x):
@@ -464,15 +500,21 @@
         functools.partial(first_kernel, frame, layers),
         in_specs=[smem, smem, smem, vmem, vmem],
         out_specs=(vmem, vmem),
-        out_shape=(packed(4, 0), tile),
+        out_shape=(
+            jax.ShapeDtypeStruct((group, 4 * frame.chunk, 128), f32) if frame.chunked else flat(4),
+            tile),
         scratch_shapes=[work],
         name="first_kernel",
-    )(device, table, gate_kinds, ket_rows, obs_rows)
+    )(device, angles, gate_kinds, ket_rows, obs_rows)
     if frame.chunked:
         got = exchange(sent)
     else:
         got = from_chunks(exchange(to_chunks(sent)))
-    outs = (packed(2, TILE),) if frame.chunked else (packed(2, TILE), tile)
+    step = 2 * frame.chunk + 1
+    if frame.chunked:
+        outs = (jax.ShapeDtypeStruct((group * step, 128), f32),)
+    else:
+        outs = (flat(2), jax.ShapeDtypeStruct((1, 128), f32))
     back = pl.pallas_call(
         functools.partial(
             middle_kernel if frame.chunked else middle_flat, frame, layers),
@@ -481,28 +523,28 @@
         out_shape=outs,
         scratch_shapes=[work],
         name="middle_kernel",
-    )(device, table, gate_kinds, got, sums)
+    )(device, angles, gate_kinds, got, sums)
     if frame.chunked:
-        final = exchange(back[0])
-        parts = jnp.zeros((1, TILE, 128), f32)
+        final = exchange(back[0].reshape(group, step, 1, 128)).reshape(group * step, 128)
+        operands = (final,)
     else:
         final = from_chunks(exchange(to_chunks(back[0])))
-        parts = lax.all_gather(back[1], "amp")
+        operands = (final, lax.all_gather(back[1], "amp"))
     bra_rows, grads = pl.pallas_call(
         functools.partial(last_kernel, frame, layers),
-        in_specs=[smem, smem, vmem, vmem],
+        in_specs=[smem, smem] + [vmem] * len(operands),
         out_specs=(vmem, smem),
         out_shape=(jax.ShapeDtypeStruct((2 * rows, 128), f32),
                    jax.ShapeDtypeStruct((layers, 3), f32)),
         scratch_shapes=[pltpu.VMEM((rows, 256), f32)],
         name="last_kernel",
-    )(table, gate_kinds, final, parts)
+    )(angles, gate_kinds, *operands)
     bra = bra_rows.reshape(rows, 2, 128).transpose(1, 0, 2).reshape(2, amp_count)
     return bra, grads
 
 
-def middle_flat(frame, layers, dev_ref, table, kinds, in_ref, sums_ref, out_ref, part_ref, work):
-    middle_kernel(frame, layers, dev_ref, table, kinds, in_ref, sums_ref, out_ref, work, part_ref)
+def middle_flat(frame, layers, dev_ref, angles, kinds, in_ref, sums_ref, out_ref, part_ref, work):
+    middle_kernel(frame, layers, dev_ref, angles, kinds, in_ref, sums_ref, out_ref, work, part_ref)
 
 
 def solution(mesh):

time: 52.2 us -> 47.4 us (0.908)
  blocking collectives: 39.6 us -> 37.4 us
  local copies, waits for them, and re-layouts: 1.94 us -> 0 us
  other arithmetic: 0.73 us -> 0 us
    all_to_all x2, blocking collectives: 39.6 us -> 37.4 us  [exchange(): return lax.all_to_all(x, 'amp', 0, 0, tiled=True)]
    unnamed x5 -> x0, local copies, waits for them, and re-layouts: 1.35 us -> none
    concatenate x1 -> x0, other arithmetic: 0.61 us -> none  [on_device(): jnp.concatenate([cosine, jnp.where(is_z, 0.0, sine), jnp.where(is_z, sine...]
    broadcast_in_dim x1 -> x0, local copies, waits for them, and re-layouts: 0.6 us -> none  [on_device(): parts = jnp.zeros((1, TILE, 128), f32)]
where the time goes in v1:
time: 47.4 us; the launch traced here: 47 us
  blocking collectives  37.4 us (79%)
  Pallas kernels  9.01 us (19%)
  between operations  0.64 us (1%)
    all_to_all x2, blocking collectives, exchange(): return lax.all_to_all(x, 'amp', 0, 0, tiled=True)  37.4 us
    pallas_call x1, Pallas kernels, on_device(): pl.pallas_call(functools.partial(middle_kernel if frame.chunked else midd...  3.87 us
    pallas_call x1, Pallas kernels, on_device(): pl.pallas_call(functools.partial(first_kernel, frame, layers), in_specs=[...  3.2 us
    pallas_call x1, Pallas kernels, on_device(): pl.pallas_call(functools.partial(last_kernel, frame, layers), in_specs=[s...  1.94 us

profile of v1, /device:TPU:0, one launch (start us, length us, event | category | flops | bytes accessed | tf_op | source)
XLA Modules:
  0.0 47.0 jit_solution(14521603718495836365)
XLA Ops:
  0.6 3.2 %first_kernel.1 = (f32[32,32,128]{2,1,0:T(8,128)}, f32[8,128]{1,0:T(8,128)}) custom-call(s32[1]{0:T(128)} %bitcast.dev_ref, f32[2,3]{1,0:T(2,128)} %angles.5, s32[2,32]{1,0:T(2,128)} %kinds.5, f32[512,128]{1,0:T(8,128)} %bitcast.16, f32[256,128]{1,0:T(8,128)} %bitcast.17), custom_call_target="tpu_custom_call" | custom-call | tf_op jit(solution)/shard_map/first_kernel/pallas_call | solution.py:499
  3.8 23.1 %all_to_all.10.in_ref = f32[32,32,128]{2,1,0:T(8,128)} all-to-all(f32[32,32,128]{2,1,0:T(8,128)} %get-tuple-element.6), channel_id=1, replica_groups=mesh['amp'=32] {'amp'}, dimensions={0} | all-to-all | bytes 1048576 | tf_op jit(solution)/shard_map/all_to_all | solution.py:486
  26.9 3.9 %middle_kernel.1 = f32[544,128]{1,0:T(8,128)} custom-call(s32[1]{0:T(128)} %bitcast.dev_ref, f32[2,3]{1,0:T(2,128)} %angles.5, s32[2,32]{1,0:T(2,128)} %kinds.5, f32[32,32,128]{2,1,0:T(8,128)} %all_to_all.10.in_ref, f32[8,128]{1,0:T(8,128)} %get-tuple-element.7.sums_ref), custom_call_target="tpu_custom_call" | custom-call | tf_op jit(solution)/shard_map/middle_kernel/pallas_call | solution.py:518
  30.8 14.4 %all_to_all.11 = f32[32,17,1,128]{3,2,1,0:T(1,128)} all-to-all(f32[32,17,1,128]{3,2,1,0:T(1,128)} %bitcast.14), channel_id=1, replica_groups=mesh['amp'=32] {'amp'}, dimensions={0} | all-to-all | bytes 557056 | tf_op jit(solution)/shard_map/all_to_all | solution.py:486
  45.1 1.9 %last_kernel.1 = (f32[512,128]{1,0:T(8,128)}, f32[2,3]{1,0:T(2,128)}) custom-call(f32[2,3]{1,0:T(2,128)} %angles.5, s32[2,32]{1,0:T(2,128)} %kinds.5, f32[544,128]{1,0:T(8,128)} %bitcast.15), custom_call_target="tpu_custom_call" | custom-call | tf_op jit(solution)/shard_map/last_kernel/pallas_call | solution.py:533

commit v2 on v1

--- a/solution.py
+++ b/solution.py
@@ -85,6 +85,20 @@
         x = x ^ x >> step
         step //= 2
     return (1 - 2 * (x & 1)).astype(jnp.float32)
+
+
+def tile_signs(frame, amp_of):
+    if frame.pivot >= ROW_BITS:
+        return [entangle(amp_of(t), frame.all_bits) for t in range(frame.tiles)]
+    edge = 1 | frame.tiles >> 1
+    made, signs = {}, []
+    for t in range(frame.tiles):
+        key = t & edge
+        if key not in made:
+            sign = entangle(amp_of(key), frame.all_bits)
+            made[key] = (sign, -sign)
+        signs.append(made[key][odd(t & t >> 1) ^ odd(key & key >> 1)])
+    return signs
 
 
 def position_index(tile):
@@ -198,19 +212,28 @@
 
 
 def lane_matrix(params, layer, qubits):
-    into = lax.broadcasted_iota(jnp.int32, (128, 128), 0)
-    out = lax.broadcasted_iota(jnp.int32, (128, 128), 1)
-    real = imag = None
+    out = lane_iota()
+    blocks = None
     for pos, qubit in enumerate(qubits):
-        c, sy, sz = [jnp.concatenate([v] * 16, axis=0) for v in params.gate(layer, qubit)]
-        z = (1 - 2 * (out >> pos & 1)).astype(jnp.float32)
-        same = (into ^ out) >> pos & 1 == 0
-        g_real = jnp.where(same, c, sy * z)
-        g_imag = jnp.where(same, sz * z, 0.0)
-        if real is None:
-            real, imag = g_real, g_imag
+        c, sy, sz = params.gate(layer, qubit)
+        upper = out >> pos & 1
+        z = (1 - 2 * upper).astype(jnp.float32)
+        y_part, z_part = sy * z, sz * z
+
+        def entry(same):
+            return jnp.where(same, c, y_part), jnp.where(same, z_part, 0.0)
+
+        if pos < 3:
+            options = [entry((sub_iota() >> pos & 1) == upper)]
         else:
-            real, imag = real * g_real - imag * g_imag, real * g_imag + imag * g_real
+            options = [entry(upper == 0), entry(upper == 1)]
+        if blocks is None:
+            blocks = options
+        else:
+            blocks = [(real * g_real - imag * g_imag, real * g_imag + imag * g_real)
+                      for g_real, g_imag in options for real, imag in blocks]
+    real = jnp.concatenate([block[0] for block in blocks], axis=0)
+    imag = jnp.concatenate([block[1] for block in blocks], axis=0)
     top = jnp.concatenate([real, imag], axis=1)
     bottom = jnp.concatenate([-imag, real], axis=1)
     return jnp.concatenate([top, bottom], axis=0)
@@ -362,34 +385,51 @@
     return load, store
 
 
-def first_kernel(frame, layers, dev_ref, angles, kinds, ket_ref, obs_ref, out_ref, sums_ref, work):
+def first_kernel(frame, layers, dev_ref, angles, kinds, ket_ref, obs_ref, out_ref, sums_ref, *scratch):
+    work, staged, done = scratch
     device = dev_ref[0]
     params = Params(angles, kinds, layers)
     layer = layers - 1
     scale = 2.0 / math.sqrt(1 << frame.all_bits)
     load_ket, store_ket = scratch_io(work, frame, 0)
     load_bra, store_bra = scratch_io(work, frame, 1)
-    for t in range(frame.tiles):
-        sign = entangle(device << frame.local_bits | position_index(t), frame.all_bits)
-        re = ket_ref[pl.ds(2 * TILE * t, TILE, stride=2), :] * sign
-        im = ket_ref[pl.ds(2 * TILE * t + 1, TILE, stride=2), :] * sign
-        store_ket(t, re, im)
-        factor = obs_ref[pl.ds(TILE * t, TILE), :] * scale
-        store_bra(t, re * factor, im * factor)
-    work[...] = lane_turn(work[...], lane_matrix(params, layer, range(LANE_BITS)))
+    signs = tile_signs(
+        frame, lambda t: device << frame.local_bits | position_index(t))
+    matrix = lane_matrix(params, layer, range(LANE_BITS))
     gates = {pos: params.gate(layer, pos) for pos in range(LANE_BITS, frame.local_bits)}
-    sweep(load_ket, store_ket, frame, gates)
-    sweep(load_bra, store_bra, frame, gates)
-    moved = list(range(frame.pivot, frame.local_bits - 1))
-    sums = gather_terms(frame, frame.first_map(), moved, load_ket, load_bra, params, device)
-    sums_ref[...] = rows_of(sums)
-    for state, load in enumerate((load_ket, load_bra)):
+    copies = []
+
+    def finish(state, load, store):
+        rows = pl.ds(state * frame.rows, frame.rows)
+        work[rows, :] = lane_turn(work[rows, :], matrix)
+        sweep(load, store, frame, gates)
         pairs = [load(t) for t in range(frame.tiles)]
         for part in range(2):
             tiles = swap_pivot([pair[part] for pair in pairs], frame)
             at = tile_ref(frame, 2 * state + part)
             for t in range(frame.tiles):
-                out_ref[at(t)] = tiles[t]
+                staged[at(t)] = tiles[t]
+        if frame.chunked:
+            span = (slice(None), pl.ds(2 * state * frame.chunk, 2 * frame.chunk))
+        else:
+            span = (pl.ds(2 * state, 2),)
+        copy = pltpu.make_async_copy(staged.at[span], out_ref.at[span], done.at[state])
+        copy.start()
+        copies.append(copy)
+
+    for t in range(frame.tiles):
+        re = ket_ref[pl.ds(2 * TILE * t, TILE, stride=2), :] * signs[t]
+        im = ket_ref[pl.ds(2 * TILE * t + 1, TILE, stride=2), :] * signs[t]
+        store_ket(t, re, im)
+        factor = obs_ref[pl.ds(TILE * t, TILE), :] * scale
+        store_bra(t, re * factor, im * factor)
+    finish(0, load_ket, store_ket)
+    finish(1, load_bra, store_bra)
+    moved = list(range(frame.pivot, frame.local_bits - 1))
+    sums = gather_terms(frame, frame.first_map(), moved, load_ket, load_bra, params, device)
+    sums_ref[...] = rows_of(sums)
+    for copy in copies:
+        copy.wait()
 
 
 def middle_kernel(frame, layers, dev_ref, angles, kinds, in_ref, sums_ref, out_ref, work, *flat_out):
@@ -414,14 +454,17 @@
     g = frame.global_bits
     high = device >> (g - 1) & 1
     base = (device & (1 << (g - 1)) - 1) << (frame.pivot + 1) | high << frame.pivot
-    for t in range(frame.tiles):
+
+    def amp_of(t):
         pos = position_index(t)
-        amp = (base | pos & (1 << frame.pivot) - 1
-               | (pos >> frame.pivot & 1) << (frame.local_bits - 1)
-               | pos >> (frame.pivot + 1) << frame.local_bits)
-        sign = entangle(amp, frame.all_bits)
+        return (base | pos & (1 << frame.pivot) - 1
+                | (pos >> frame.pivot & 1) << (frame.local_bits - 1)
+                | pos >> (frame.pivot + 1) << frame.local_bits)
+
+    signs = tile_signs(frame, amp_of)
+    for t in range(frame.tiles):
         re, im = load_bra(t)
-        store_bra(t, re * sign, im * sign)
+        store_bra(t, re * signs[t], im * signs[t])
     bra_rows = pl.ds(frame.rows, frame.rows)
     lane_on = [placed[pos] for pos in range(LANE_BITS)]
     work[bra_rows, :] = lane_turn(work[bra_rows, :], lane_matrix(params, 0, lane_on))
@@ -496,14 +539,15 @@
     obs_rows = observable.reshape(rows, 128)
     work = pltpu.VMEM((2 * rows, 256), f32)
     tile = jax.ShapeDtypeStruct((TILE, 128), f32)
+    sent_shape = flat(4)
+    if frame.chunked:
+        sent_shape = jax.ShapeDtypeStruct((group, 4 * frame.chunk, 128), f32)
     sent, sums = pl.pallas_call(
         functools.partial(first_kernel, frame, layers),
         in_specs=[smem, smem, smem, vmem, vmem],
-        out_specs=(vmem, vmem),
-        out_shape=(
-            jax.ShapeDtypeStruct((group, 4 * frame.chunk, 128), f32) if frame.chunked else flat(4),
-            tile),
-        scratch_shapes=[work],
+        out_specs=(pl.BlockSpec(memory_space=pl.ANY), vmem),
+        out_shape=(sent_shape, tile),
+        scratch_shapes=[work, pltpu.VMEM(sent_shape.shape, f32), pltpu.SemaphoreType.DMA((2,))],
         name="first_kernel",
     )(device, angles, gate_kinds, ket_rows, obs_rows)
     if frame.chunked:

time: 47.4 us -> 47.7 us (level)
    pallas_call x1, Pallas kernels: 3.2 us -> 3.71 us  [on_device(): pl.pallas_call(functools.partial(first_kernel, frame, layers), in_specs=[...]
where the time goes in v2:
time: 47.7 us; the launch traced here: 47.4 us
  blocking collectives  37.4 us (78%)
  Pallas kernels  9.3 us (19%)
  between operations  0.64 us (1%)
    all_to_all x2, blocking collectives, exchange(): return lax.all_to_all(x, 'amp', 0, 0, tiled=True)  37.4 us
    pallas_call x1, Pallas kernels, on_device(): pl.pallas_call(functools.partial(first_kernel, frame, layers), in_specs=[...  3.71 us
    pallas_call x1, Pallas kernels, on_device(): pl.pallas_call(functools.partial(middle_kernel if frame.chunked else midd...  3.65 us
    pallas_call x1, Pallas kernels, on_device(): pl.pallas_call(functools.partial(last_kernel, frame, layers), in_specs=[s...  1.94 us

profile of v2, /device:TPU:0, one launch (start us, length us, event | category | flops | bytes accessed | tf_op | source)
XLA Modules:
  0.0 47.4 jit_solution(6597307437935552954)
XLA Ops:
  0.6 3.7 %first_kernel.1 = (f32[32,32,128]{2,1,0:T(8,128)}, f32[8,128]{1,0:T(8,128)}) custom-call(s32[1]{0:T(128)} %bitcast.dev_ref, f32[2,3]{1,0:T(2,128)} %angles.5, s32[2,32]{1,0:T(2,128)} %kinds.5, f32[512,128]{1,0:T(8,128)} %bitcast.16, f32[256,128]{1,0:T(8,128)} %bitcast.17), custom_call_target="tpu_custom_call" | custom-call | tf_op jit(solution)/shard_map/first_kernel/pallas_call | solution.py:545
  4.3 23.1 %all_to_all.10.in_ref = f32[32,32,128]{2,1,0:T(8,128)} all-to-all(f32[32,32,128]{2,1,0:T(8,128)} %get-tuple-element.6), channel_id=1, replica_groups=mesh['amp'=32] {'amp'}, dimensions={0} | all-to-all | bytes 1048576 | tf_op jit(solution)/shard_map/all_to_all | solution.py:529
  27.4 3.6 %middle_kernel.1 = f32[544,128]{1,0:T(8,128)} custom-call(s32[1]{0:T(128)} %bitcast.dev_ref, f32[2,3]{1,0:T(2,128)} %angles.5, s32[2,32]{1,0:T(2,128)} %kinds.5, f32[32,32,128]{2,1,0:T(8,128)} %all_to_all.10.in_ref, f32[8,128]{1,0:T(8,128)} %get-tuple-element.7.sums_ref), custom_call_target="tpu_custom_call" | custom-call | tf_op jit(solution)/shard_map/middle_kernel/pallas_call | solution.py:562
  31.1 14.4 %all_to_all.11 = f32[32,17,1,128]{3,2,1,0:T(1,128)} all-to-all(f32[32,17,1,128]{3,2,1,0:T(1,128)} %bitcast.14), channel_id=1, replica_groups=mesh['amp'=32] {'amp'}, dimensions={0} | all-to-all | bytes 557056 | tf_op jit(solution)/shard_map/all_to_all | solution.py:529
  45.4 1.9 %last_kernel.1 = (f32[512,128]{1,0:T(8,128)}, f32[2,3]{1,0:T(2,128)}) custom-call(f32[2,3]{1,0:T(2,128)} %angles.5, s32[2,32]{1,0:T(2,128)} %kinds.5, f32[544,128]{1,0:T(8,128)} %bitcast.15), custom_call_target="tpu_custom_call" | custom-call | tf_op jit(solution)/shard_map/last_kernel/pallas_call | solution.py:577
